TPU v7x, 16 devices: a 4x2x1 block of a 4x4x8 slice. The times are simulated.
16 devices in a mesh: dp: 4 (over y, z, core), sp: 4 (over x).
Axes of the slice: x: 4, y: 2, z: 1, core: 2. Of those that a mesh axis runs over, the one named last changes fastest.
The devices are a block of a 4x4x8 slice.
Arguments:
- q: bfloat16 [128, 48, 128], P('dp'), parts along dimension 0
- k: bfloat16 [128, 8192, 4, 128], P('dp', 'sp'), parts along dimension 0
- v: bfloat16 [128, 8192, 4, 128], P('dp', 'sp'), parts along dimension 0
Outputs:
- q: bfloat16 [128, 48, 128], P('dp'), parts along dimension 0
There are 4 independent parts. A program takes and returns all parts, laid end to end along the dimension named above; each array names one.
All inputs are finite; a program needn't handle non-finite values.
Results may differ from a plain program's by a relative error of at most 0.012.
Values are sent between devices in bfloat16 or wider.
A program may use at most 768 MiB of HBM per device.

v0:
```python
import jax
import jax.numpy as jnp
from jax import lax
from jax.sharding import PartitionSpec as P


def einsum(form, a, b):
    return jnp.einsum(form, a.astype(jnp.float32), b.astype(jnp.float32))


def part_of(q, k, v):
    grouped = q.reshape(q.shape[0], k.shape[2], -1, q.shape[2])
    scores = einsum("bgsd,bugd->bgsu", grouped, k) * q.shape[2] ** -0.5
    high = jnp.max(scores, -1, keepdims=True)
    weights = jnp.exp(scores - high)
    seen = einsum("bgsu,bugd->bgsd", weights.astype(jnp.bfloat16), v)
    return jnp.concatenate([seen, jnp.sum(weights, -1, keepdims=True), high], -1)


def together(parts):
    seen, total, high = parts[..., :-2], parts[..., -2:-1], parts[..., -1:]
    scale = jnp.exp(high - jnp.max(high, 0))
    return (jnp.sum(seen * scale, 0) / jnp.sum(total * scale, 0)).astype(jnp.bfloat16)


def solution(mesh):
    def step(q, k, v):
        return together(lax.all_gather(part_of(q, k, v), "sp")).reshape(q.shape)

    return jax.shard_map(
        step,
        mesh=mesh,
        in_specs=(P("dp", None, None), P("dp", "sp", None, None), P("dp", "sp", None, None)),
        out_specs=P("dp", None, None),
        check_vma=False,
    )
```

profile of v0, /device:TPU:112, one launch (start us, length us, event | category | flops | bytes accessed | tf_op | source)
XLA Modules:
  0.0 182.1 jit_solution(1020646524828352167)
XLA Ops:
  6.5 0.0 all-gather.3.cloned.1.call-start
  6.6 1.1 copy.17
  7.7 34.9 %multiply_reduce_fusion = (f32[32,4,12]{2,1,0:T(4,128)S(1)}, f32[32,4,12,2048]{3,2,1,0:T(8,128)}) fusion(bf16[32,2048,4,128]{3,2,1,0:T(4,128)(2,1)} %param.4, bf16[32,4,12,128]{3,0,2,1:T(8,128)(2,1)S(1)} %bitcast.14), kind=kOutput, calls=%fused_computation.5 | convolution fusion | flops 811596288 | bytes 80091136 | tf_op jit(solution)/shard_map/bgsd,bugd->bgsu/dot_general | solution.py:8
  42.5 7.7 %fusion.4 = f32[32,4,12]{2,1,0:T(4,128)S(1)} fusion(f32[32,4,12,2048]{3,2,1,0:T(8,128)} %get-tuple-element.11, f32[32,4,12]{2,1,0:T(4,128)S(1)} %get-tuple-element.10), kind=kLoop, calls=%fused_computation.6 | loop fusion | flops 9435648 | bytes 12595200 | tf_op jit(solution)/shard_map/reduce_sum | solution.py:17
  50.3 34.4 %fusion = f32[32,4,12,128]{3,2,1,0:T(8,128)S(1)} fusion(bf16[32,2048,4,128]{3,2,1,0:T(4,128)(2,1)} %param.5, f32[32,4,12,2048]{3,2,1,0:T(8,128)} %get-tuple-element.11, f32[32,4,12]{2,1,0:T(4,128)S(1)} %get-tuple-element.10), kind=kOutput, calls=%fused_computation | convolution fusion | flops 814743552 | bytes 80484352 | tf_op jit(solution)/shard_map/bgsu,bugd->bgsd/dot_general | solution.py:8
  84.6 0.9 copy.23
  85.5 0.9 copy.24
  86.4 0.4 pad_maximum_fusion
  86.8 2.5 %copy.25 = f32[32,4,12,130]{3,1,2,0:T(4,128)} copy(f32[32,4,12,130]{3,2,1,0:T(8,128)S(1)} %pad_maximum_fusion) | data formatting | bytes 1597440 | tf_op jit(solution)/shard_map/concatenate | solution.py:17
  89.3 0.1 all-gather.3.cloned.1.call-update
  89.4 64.6 %all-gather.3.cloned.1.call-done = f32[128,4,12,130]{3,1,2,0:T(4,128)} async-done(((f32[32,4,12,130]{3,1,2,0:T(4,128)}), f32[128,4,12,130]{3,1,2,0:T(4,128)}) %all-gather.3.cloned.1.call-update) | async-done | bytes 3194896 | tf_op jit(solution)/shard_map/all_gather | solution.py:28
  154.0 2.1 %slice.12 = f32[4,32,4,12,128]{4,2,3,1,0:T(4,128)S(1)} slice(f32[4,32,4,12,130]{4,2,3,1,0:T(4,128)} %bitcast.12), slice={[0:4], [0:32], [0:4], [0:12], [0:128]} | slice | bytes 6291456 | tf_op jit(solution)/shard_map/slice | solution.py:21
  156.2 7.2 %fusion.14 = (f32[4,32,4,12,1]{4,2,3,1,0:T(4,128)}, f32[32,4,12]{1,2,0:T(8,128)S(1)}, f32[4,32,4,12,1]{4,2,3,1,0:T(4,128)}) fusion(f32[4,32,4,12,130]{4,2,3,1,0:T(4,128)} %bitcast.13), kind=kLoop, calls=%fused_computation.21 | loop fusion | flops 4608 | bytes 104448 | tf_op jit(solution)/shard_map/slice | solution.py:21
  163.4 3.4 %copy.39 = f32[4,32,4,12,1]{1,2,3,0,4:T(4,128)S(1)} copy(f32[4,32,4,12,1]{4,2,3,1,0:T(4,128)} %get-tuple-element.5) | data formatting | bytes 49152
  166.8 0.2 copy.40
  167.0 3.4 %copy.38 = f32[4,32,4,12,1]{1,2,3,0,4:T(4,128)S(1)} copy(f32[4,32,4,12,1]{4,2,3,1,0:T(4,128)} %get-tuple-element.7) | data formatting | bytes 49152
  170.4 0.7 multiply_reduce_fusion.1
  171.2 1.1 copy.28
  172.2 1.3 fusion.9
  173.6 0.5 copy.29
  174.0 0.3 fusion.10
  174.3 0.9 copy.32
  (2 shorter events, 0.0 us)
Async XLA Ops:
  6.5 147.5 %all-gather.3.cloned.1.call-start = ((), (), s32[]{:S(2)}) async-start(), calls=%async_computation | async-start | bytes 7864320 | tf_op jit(solution)/shard_map/all_gather | solution.py:28
Sparse Core Ops, SparseCore 0:
  89.5 64.4 all-gather.2
where the time goes:
time: 183 us; the launch traced here: 182 us
  matrix products  69.2 us (38%)
  waiting for transfers between devices  64.7 us (35%)
  other arithmetic  17.7 us (10%)
  local copies, waits for them, and re-layouts  17 us (9%)
  between operations  13.5 us (7%)
    dot_general x2, matrix products, einsum(): return jnp.einsum(form, a.astype(jnp.float32), b.astype(jnp.float32))  69.2 us
    all_gather x1, waiting for transfers between devices, step(): return together(lax.all_gather(part_of(q, k, v), 'sp')).reshape(q.shape)  64.6 us
    unnamed x4, local copies, waits for them, and re-layouts  8.14 us
    reduce_sum x1, other arithmetic, part_of(): jnp.sum(weights, -1, keepdims=True)  7.71 us
    slice x1, other arithmetic, together(): seen, total, high = (parts[..., :-2], parts[..., -2:-1], parts[..., -1:])  7.22 us
  transfers between devices with their start and end apart: 1, of which 1 were waited for; matrix products, arithmetic and copies ran while one was open for 0% of the time, Pallas kernels for 0%

commit v1 on v0

v1 whole, which is shorter than its diff:
```python
import functools
import math

import jax
import jax.numpy as jnp
from jax import lax
from jax.experimental import pallas as pl
from jax.experimental.pallas import tpu as pltpu
from jax.sharding import PartitionSpec as P

MESH = pl.DeviceIdType.MESH
F32, BF16 = jnp.float32, jnp.bfloat16
SLOTS = 6
LAG = 4
TILE = 256


def lane_fold(x, op):
    for shift in (4, 8, 16, 32, 64):
        x = op(x, pltpu.roll(x, shift, 1))
    return x


def kernel(n, heads_kv, q_hbm, k_hbm, v_hbm, out_ref, qbuf, kbuf, vbuf, s0, s1, h0, h1, m0, m1, l0, l1, mask_ref, part, stat, qsem, ksem, vsem,
           part_send, part_recv, stat_send, stat_recv):
    me = lax.axis_index("sp")
    batch, heads, head = qbuf.shape
    slots, rows = kbuf.shape[:2]
    half = rows // 2
    tiles = half // TILE
    factor = head**-0.5 * math.log2(math.e)
    groups = batch // 2 - 1

    def k_copy(i):
        slot = lax.rem(i, slots)
        return pltpu.make_async_copy(k_hbm.at[i], kbuf.at[slot], ksem.at[slot])

    def v_copy(i):
        slot = lax.rem(i, slots)
        return pltpu.make_async_copy(v_hbm.at[i], vbuf.at[slot], vsem.at[slot])

    def transfers(g, first, count):
        out = []
        for off in (1, n - 1, *range(2, n - 1)):
            to = {"sp": lax.rem(me + off, n)}
            for buf, ssem, rsem in ((part, part_send, part_recv), (stat, stat_send, stat_recv)):
                ref = buf.at[me, pl.ds(first, count)]
                out.append(pltpu.make_async_remote_copy(ref, ref, ssem.at[g, off - 1], rsem.at[g, off - 1], device_id=to, device_id_type=MESH))
        return out

    def arrivals(g, first, count):
        out = []
        for off in range(1, n):
            src = lax.rem(me + n - off, n)
            for buf, ssem, rsem in ((part, part_send, part_recv), (stat, stat_send, stat_recv)):
                ref = buf.at[src, pl.ds(first, count)]
                out.append(pltpu.make_async_remote_copy(ref, ref, ssem.at[g, off - 1], rsem.at[g, off - 1], device_id={"sp": src}, device_id_type=MESH))
        return out

    q_copy = pltpu.make_async_copy(q_hbm, qbuf, qsem)
    q_copy.start()
    for i in range(slots - 1):
        k_copy(i).start()
        if i < slots - 2:
            v_copy(i).start()

    barrier = pltpu.get_barrier_semaphore()
    for off in range(1, n):
        pl.semaphore_signal(barrier, inc=1, device_id={"sp": lax.rem(me + off, n)}, device_id_type=MESH)

    per = heads // heads_kv
    own = lax.broadcasted_iota(jnp.int32, (heads, TILE), 0) // per == lax.rem(lax.broadcasted_iota(jnp.int32, (heads, TILE), 1), heads_kv)
    mask_ref[...] = jnp.where(own, 1.0, 0.0).astype(BF16)
    kind = lax.rem(lax.broadcasted_iota(jnp.int32, (8, TILE), 1), heads_kv)
    lane = lax.broadcasted_iota(jnp.int32, (8, 128), 1)
    low = lax.broadcasted_iota(jnp.int32, (8, 128), 0) < 4

    def scores(i, s_ref, h_ref):
        slot = lax.rem(i, slots)
        q = qbuf[i]
        zero = jnp.zeros_like(q)
        lhs = jnp.concatenate([jnp.concatenate([q, zero], 1), jnp.concatenate([zero, q], 1)], 0)
        top = None
        for c in range(tiles):
            lanes = slice(c * TILE, (c + 1) * TILE)
            rhs = jnp.concatenate([kbuf[slot, c * TILE : (c + 1) * TILE, :], kbuf[slot, half + c * TILE : half + (c + 1) * TILE, :]], 1)
            s = lax.dot_general(lhs, rhs, (((1,), (1,)), ((), ())), preferred_element_type=F32)
            for x in range(2):
                r = s[heads * x : heads * (x + 1)]
                a = jnp.where(kind == 0, r[0:8], jnp.where(kind == 1, r[16:24], jnp.where(kind == 2, r[24:32], r[40:48])))
                b = jnp.where(kind < 2, r[8:16], r[32:40])
                s_ref[x, 0:8, lanes] = a
                s_ref[x, 8:16, lanes] = b
                top = (a, b) if top is None else (jnp.maximum(top[0], a), jnp.maximum(top[1], b))
            if c % 2:
                yield
        for x in range(2):
            h_ref[x] = jnp.maximum(top[x][:, :128], top[x][:, 128:])

    def weigh(i, s_ref, h_ref, m_ref, l_ref):
        slot = lax.rem(i, slots)
        high = [lane_fold(h_ref[x], jnp.maximum) for x in range(2)]
        for x in range(2):
            m_ref[x] = high[x]
        yield
        wide = [jnp.concatenate([h, h], 1) for h in high]
        sums = [jnp.zeros((8, TILE), F32), jnp.zeros((8, TILE), F32)]
        acc = [None, None]
        mask = mask_ref[...]
        for c in range(tiles):
            lanes = slice(c * TILE, (c + 1) * TILE)
            both = []
            for x in range(2):
                a = jnp.exp2((s_ref[x, 0:8, lanes] - wide[0]) * factor)
                b = jnp.exp2((s_ref[x, 8:16, lanes] - wide[1]) * factor)
                sums = [sums[0] + a, sums[1] + b]
                both.append(jnp.concatenate([a, b, a, a, b, a], 0).astype(BF16) * mask)
            w = jnp.concatenate(both, 0)
            rhs = jnp.concatenate([vbuf[slot, c * TILE : (c + 1) * TILE, :], vbuf[slot, half + c * TILE : half + (c + 1) * TILE, :]], 1)
            o = jnp.dot(w, rhs, preferred_element_type=F32)
            acc[c % 2] = o if acc[c % 2] is None else acc[c % 2] + o
            if c % 2:
                yield
        o = acc[0] + acc[1]
        part[me, i] = (o[:heads, :head] + o[heads:, head:]).astype(BF16)
        for x in range(2):
            l_ref[x] = sums[x][:, :128] + sums[x][:, 128:]

    def settle(i, m_ref, l_ref):
        sums = [lane_fold(l_ref[x], jnp.add) for x in range(2)]
        stat[me, i] = jnp.where(lane < 32, m_ref[0], jnp.where(lane < 64, m_ref[1], jnp.where(lane < 96, sums[0], sums[1])))
        yield

    def run(*gens):
        gens = list(gens)
        while gens:
            for g in list(gens):
                try:
                    next(g)
                except StopIteration:
                    gens.remove(g)

    def combine(i):
        st = [stat[p, i] for p in range(n)]
        top = functools.reduce(jnp.maximum, st)
        scale = [jnp.exp2((s - top) * factor) for s in st]
        total = sum(w * pltpu.roll(s, 64, 1) for w, s in zip(scale, st))
        inv = 1.0 / total
        yield
        acc = None
        for p in range(n):
            w = scale[p] * inv

            def col(c):
                return jnp.broadcast_to(w[:, c : c + 1], (8, head))

            m01 = jnp.where(low, col(32), col(33))
            m23 = jnp.where(low, col(34), col(35))
            full = jnp.concatenate([col(0), m01, col(1), col(2), m23, col(3)], 0)
            term = part[p, i].astype(F32) * full
            acc = term if acc is None else acc + term
            yield
        out_ref[i] = acc.astype(BF16)

    def wait_arrivals(g, first, count):
        for c in arrivals(g, first, count):
            c.wait_recv()

    def send(g, first, count):
        for c in transfers(g, first, count):
            c.start()

    def wait_sent(g, first, count):
        for c in transfers(g, first, count):
            c.wait_send()

    q_copy.wait()
    k_copy(0).wait()
    run(scores(0, s0, h0))
    pl.semaphore_wait(barrier, n - 1)

    def body(full, j, _):
        for copy, i in ((k_copy, 2 * j - 1 + slots), (v_copy, 2 * j - 2 + slots), (k_copy, 2 * j + slots), (v_copy, 2 * j - 1 + slots)):
            @pl.when(i < batch)
            def _():
                copy(i).start()

        extra = []
        if full:
            wait_arrivals(j - LAG, 2 * (j - LAG), 2)
            wait_sent(j - LAG, 2 * (j - LAG), 2)
            send(j - 2, 2 * (j - 2), 2)
            extra = [combine(2 * (j - LAG)), combine(2 * (j - LAG) + 1)]
        else:
            @pl.when(j >= 2)
            def _():
                send(j - 2, 2 * (j - 2), 2)

        k_copy(2 * j + 1).wait()
        v_copy(2 * j).wait()
        k_copy(2 * j + 2).wait()
        v_copy(2 * j + 1).wait()
        run(scores(2 * j + 1, s1, h1), weigh(2 * j, s0, h0, m0, l0), settle(lax.max(2 * j - 1, 0), m1, l1), *extra[:1])
        run(scores(2 * j + 2, s0, h0), weigh(2 * j + 1, s1, h1, m1, l1), settle(2 * j, m0, l0), *extra[1:])
        return 0

    lax.fori_loop(0, LAG, functools.partial(body, False), 0)
    lax.fori_loop(LAG, groups, functools.partial(body, True), 0)
    last = batch - 1
    before = (groups - 2, 2 * (groups - 2), 2)
    sent = [(groups - 1, 2 * (groups - 1), 2), (groups, last - 1, 1), (groups + 1, last, 1)]
    send(*before)
    k_copy(last).wait()
    v_copy(last - 1).wait()
    run(scores(last, s1, h1), weigh(last - 1, s0, h0, m0, l0), settle(last - 2, m1, l1))
    send(*sent[0])
    run(settle(last - 1, m0, l0))
    send(*sent[1])
    v_copy(last).wait()
    run(weigh(last, s1, h1, m1, l1))
    run(settle(last, m1, l1))
    send(*sent[2])

    def rest(g, _):
        wait_arrivals(g, 2 * g, 2)
        wait_sent(g, 2 * g, 2)
        run(combine(2 * g), combine(2 * g + 1))
        return 0

    lax.fori_loop(groups - LAG, groups, rest, 0)
    for s in sent[1:]:
        wait_arrivals(*s)
        run(combine(s[1]))
    for s in sent[1:]:
        wait_sent(*s)


def solution(mesh):
    n = mesh.shape["sp"]

    def step(q, k, v):
        batch, heads, head = q.shape
        tokens, heads_kv = k.shape[1:3]
        rows = tokens * heads_kv
        groups = batch // 2 + 1
        any_spec = pl.BlockSpec(memory_space=pl.ANY)
        return pl.pallas_call(
            functools.partial(kernel, n, heads_kv),
            out_shape=jax.ShapeDtypeStruct(q.shape, BF16),
            in_specs=[any_spec] * 3,
            out_specs=pl.BlockSpec(memory_space=pltpu.VMEM),
            scratch_shapes=[
                pltpu.VMEM((batch, heads, head), BF16),
                pltpu.VMEM((SLOTS, rows, head), BF16),
                pltpu.VMEM((SLOTS, rows, head), BF16),
                pltpu.VMEM((2, 16, rows // 2), F32),
                pltpu.VMEM((2, 16, rows // 2), F32),
                *[pltpu.VMEM((2, 8, 128), F32)] * 6,
                pltpu.VMEM((heads, TILE), BF16),
                pltpu.VMEM((n, batch, heads, head), BF16),
                pltpu.VMEM((n, batch, 8, 128), F32),
                pltpu.SemaphoreType.DMA,
                pltpu.SemaphoreType.DMA((SLOTS,)),
                pltpu.SemaphoreType.DMA((SLOTS,)),
                pltpu.SemaphoreType.DMA((groups, n - 1)),
                pltpu.SemaphoreType.DMA((groups, n - 1)),
                pltpu.SemaphoreType.DMA((groups, n - 1)),
                pltpu.SemaphoreType.DMA((groups, n - 1)),
            ],
            compiler_params=pltpu.CompilerParams(collective_id=0, has_side_effects=True, vmem_limit_bytes=60 * 2**20),
        )(q, k.reshape(batch, rows, head), v.reshape(batch, rows, head))

    return jax.shard_map(
        step,
        mesh=mesh,
        in_specs=(P("dp", None, None), P("dp", "sp", None, None), P("dp", "sp", None, None)),
        out_specs=P("dp", None, None),
        check_vma=False,
    )
```

time: 183 us -> 57 us (0.31)
  matrix products: 69.2 us -> 0 us
  waiting for transfers between devices: 64.7 us -> 0 us
  Pallas kernels: 0 us -> 55.1 us
  other arithmetic: 17.7 us -> 0 us
  local copies, waits for them, and re-layouts: 17 us -> 1.77 us
  between operations: 13.5 us -> 0.01 us
    dot_general x2 -> x0, matrix products: 69.2 us -> none  [einsum(): return jnp.einsum(form, a.astype(jnp.float32), b.astype(jnp.float32))]
    all_gather x1 -> x0, waiting for transfers between devices: 64.6 us -> none  [step(): return together(lax.all_gather(part_of(q, k, v), 'sp')).reshape(q.shape)]
    pallas_call x0 -> x1, Pallas kernels: none -> 55.1 us  [step(): pl.pallas_call(functools.partial(kernel, n, heads_kv), out_shape=jax.Shap...]
    reduce_sum x3 -> x0, other arithmetic: 9.74 us -> none  [the longest x1 7.71 us: part_of(): jnp.sum(weights, -1, keepdims=True)]
    slice x1 -> x0, other arithmetic: 7.22 us -> none  [together(): seen, total, high = (parts[..., :-2], parts[..., -2:-1], parts[..., -1:])]
    unnamed x4 -> x1, local copies, waits for them, and re-layouts: 8.14 us -> 1.77 us
    concatenate x1 -> x0, local copies, waits for them, and re-layouts: 2.49 us -> none  [part_of(): jnp.concatenate([seen, jnp.sum(weights, -1, keepdims=True), high], -1)]
    slice x1 -> x0, local copies, waits for them, and re-layouts: 2.14 us -> none  [together(): seen, total, high = (parts[..., :-2], parts[..., -2:-1], parts[..., -1:])]
  transfers between devices with their start and end apart: 1 -> 0, of which waited for: 1 -> 0; matrix products, arithmetic and copies ran while one was open for 0% -> 0% of each run, Pallas kernels for 0% -> 0%
where the time goes in v1:
time: 57 us; the launch traced here: 56.9 us
  Pallas kernels  55.1 us (97%)
  local copies, waits for them, and re-layouts  1.77 us (3%)
    pallas_call x1, Pallas kernels, step(): pl.pallas_call(functools.partial(kernel, n, heads_kv), out_shape=jax.Shap...  55.1 us
    unnamed x1, local copies, waits for them, and re-layouts  1.77 us

profile of v1, /device:TPU:112, one launch (start us, length us, event | category | flops | bytes accessed | tf_op | source)
XLA Modules:
  0.0 56.9 jit_solution(9716458016099744659)
XLA Ops:
  0.0 55.1 %shard_map.37 = bf16[32,48,128]{2,1,0:T(8,128)(2,1)} custom-call(bf16[32,48,128]{2,1,0:T(8,128)(2,1)} %q_hbm.1, bf16[32,8192,128]{2,1,0:T(8,128)(2,1)} %bitcast.k_hbm, bf16[32,8192,128]{2,1,0:T(8,128)(2,1)} %bitcast.1.v_hbm), custom_call_target="tpu_custom_call" | custom-call | tf_op jit(solution)/shard_map/pallas_call | solution.py:247
  55.1 1.8 %copy.5 = bf16[32,48,128]{2,1,0:T(8,128)(2,1)} copy(bf16[32,48,128]{2,1,0:T(8,128)(2,1)} %shard_map.37) | data formatting | bytes 786432

commit v2 on v1

--- a/solution.py
+++ b/solution.py
@@ -12,13 +12,16 @@
 F32, BF16 = jnp.float32, jnp.bfloat16
 SLOTS = 6
 LAG = 4
+LEAD = 4
 TILE = 256
 
 
-def lane_fold(x, op):
-    for shift in (4, 8, 16, 32, 64):
-        x = op(x, pltpu.roll(x, shift, 1))
-    return x
+def lane_fold(x, kind, kinds, reduce, fill):
+    out = None
+    for g in range(kinds):
+        r = reduce(jnp.where(kind == g, x, fill), axis=1, keepdims=True)
+        out = jnp.broadcast_to(r, x.shape) if out is None else jnp.where(kind == g, r, out)
+    return out
 
 
 def kernel(n, heads_kv, q_hbm, k_hbm, v_hbm, out_ref, qbuf, kbuf, vbuf, s0, s1, h0, h1, m0, m1, l0, l1, mask_ref, part, stat, qsem, ksem, vsem,
@@ -59,10 +62,10 @@
 
     q_copy = pltpu.make_async_copy(q_hbm, qbuf, qsem)
     q_copy.start()
-    for i in range(slots - 1):
+    k_copy(0).start()
+    for i in range(1, slots):
         k_copy(i).start()
-        if i < slots - 2:
-            v_copy(i).start()
+        v_copy(i - 1).start()
 
     barrier = pltpu.get_barrier_semaphore()
     for off in range(1, n):
@@ -99,7 +102,7 @@
 
     def weigh(i, s_ref, h_ref, m_ref, l_ref):
         slot = lax.rem(i, slots)
-        high = [lane_fold(h_ref[x], jnp.maximum) for x in range(2)]
+        high = [lane_fold(h_ref[x], kind[:, :128], heads_kv, jnp.max, -jnp.inf) for x in range(2)]
         for x in range(2):
             m_ref[x] = high[x]
         yield
@@ -127,7 +130,7 @@
             l_ref[x] = sums[x][:, :128] + sums[x][:, 128:]
 
     def settle(i, m_ref, l_ref):
-        sums = [lane_fold(l_ref[x], jnp.add) for x in range(2)]
+        sums = [lane_fold(l_ref[x], kind[:, :128], heads_kv, jnp.sum, 0.0) for x in range(2)]
         stat[me, i] = jnp.where(lane < 32, m_ref[0], jnp.where(lane < 64, m_ref[1], jnp.where(lane < 96, sums[0], sums[1])))
         yield
 
@@ -139,6 +142,23 @@
                     next(g)
                 except StopIteration:
                     gens.remove(g)
+
+    def block(first, second, *others):
+        others = list(others)
+
+        def step(g, count=1):
+            for _ in range(count):
+                next(g, None)
+
+        step(second)
+        step(first, LEAD)
+        while True:
+            for g in others:
+                step(g)
+            step(second, 2)
+            if next(first, StopIteration) is StopIteration:
+                break
+        run(second, *others)
 
     def combine(i):
         st = [stat[p, i] for p in range(n)]
@@ -179,12 +199,15 @@
     run(scores(0, s0, h0))
     pl.semaphore_wait(barrier, n - 1)
 
+    def fetch(i):
+        for copy, later in ((k_copy, i + slots), (v_copy, i + slots - 1)):
+            @pl.when(later < batch)
+            def _():
+                copy(later).start()
+
     def body(full, j, _):
-        for copy, i in ((k_copy, 2 * j - 1 + slots), (v_copy, 2 * j - 2 + slots), (k_copy, 2 * j + slots), (v_copy, 2 * j - 1 + slots)):
-            @pl.when(i < batch)
-            def _():
-                copy(i).start()
-
+        i = 2 * j
+        fetch(i)
         extra = []
         if full:
             wait_arrivals(j - LAG, 2 * (j - LAG), 2)
@@ -196,12 +219,13 @@
             def _():
                 send(j - 2, 2 * (j - 2), 2)
 
-        k_copy(2 * j + 1).wait()
-        v_copy(2 * j).wait()
-        k_copy(2 * j + 2).wait()
-        v_copy(2 * j + 1).wait()
-        run(scores(2 * j + 1, s1, h1), weigh(2 * j, s0, h0, m0, l0), settle(lax.max(2 * j - 1, 0), m1, l1), *extra[:1])
-        run(scores(2 * j + 2, s0, h0), weigh(2 * j + 1, s1, h1, m1, l1), settle(2 * j, m0, l0), *extra[1:])
+        k_copy(i + 1).wait()
+        v_copy(i).wait()
+        block(scores(i + 1, s1, h1), weigh(i, s0, h0, m0, l0), settle(lax.max(i - 1, 0), m1, l1), *extra[:1])
+        fetch(i + 1)
+        k_copy(i + 2).wait()
+        v_copy(i + 1).wait()
+        block(scores(i + 2, s0, h0), weigh(i + 1, s1, h1, m1, l1), settle(i, m0, l0), *extra[1:])
         return 0
 
     lax.fori_loop(0, LAG, functools.partial(body, False), 0)
@@ -209,11 +233,12 @@
     last = batch - 1
     before = (groups - 2, 2 * (groups - 2), 2)
     sent = [(groups - 1, 2 * (groups - 1), 2), (groups, last - 1, 1), (groups + 1, last, 1)]
+    k_copy(last).wait()
+    run(scores(last, s1, h1), settle(last - 2, m1, l1))
     send(*before)
-    k_copy(last).wait()
+    send(*sent[0])
     v_copy(last - 1).wait()
-    run(scores(last, s1, h1), weigh(last - 1, s0, h0, m0, l0), settle(last - 2, m1, l1))
-    send(*sent[0])
+    run(weigh(last - 1, s0, h0, m0, l0))
     run(settle(last - 1, m0, l0))
     send(*sent[1])
     v_copy(last).wait()
@@ -246,7 +271,7 @@
         any_spec = pl.BlockSpec(memory_space=pl.ANY)
         return pl.pallas_call(
             functools.partial(kernel, n, heads_kv),
-            out_shape=jax.ShapeDtypeStruct(q.shape, BF16),
+            out_shape=pltpu.VMEM(q.shape, BF16),
             in_specs=[any_spec] * 3,
             out_specs=pl.BlockSpec(memory_space=pltpu.VMEM),
             scratch_shapes=[
@@ -267,8 +292,8 @@
                 pltpu.SemaphoreType.DMA((groups, n - 1)),
                 pltpu.SemaphoreType.DMA((groups, n - 1)),
             ],
-            compiler_params=pltpu.CompilerParams(collective_id=0, has_side_effects=True, vmem_limit_bytes=60 * 2**20),
-        )(q, k.reshape(batch, rows, head), v.reshape(batch, rows, head))
+            compiler_params=pltpu.CompilerParams(collective_id=0, has_side_effects=True, vmem_limit_bytes=48 * 2**20),
+        )(pltpu.with_memory_space_constraint(q, pltpu.HBM), k.reshape(batch, rows, head), v.reshape(batch, rows, head))
 
     return jax.shard_map(
         step,

time: 57 us -> 54 us (0.947)
  Pallas kernels: 55.1 us -> 53.2 us
  local copies, waits for them, and re-layouts: 1.77 us -> 0.75 us
    pallas_call x1, Pallas kernels: 55.1 us -> 53.2 us  [step(): pl.pallas_call(functools.partial(kernel, n, heads_kv), out_shape=pltpu.VM...]
    unnamed x1, local copies, waits for them, and re-layouts: 1.77 us -> 0.75 us
where the time goes in v2:
time: 54 us
  Pallas kernels  53.2 us (99%)
  local copies, waits for them, and re-layouts  0.75 us (1%)
    pallas_call x1, Pallas kernels, step(): pl.pallas_call(functools.partial(kernel, n, heads_kv), out_shape=pltpu.VM...  53.2 us

profile of v2, /device:TPU:112, one launch (start us, length us, event | category | flops | bytes accessed | tf_op | source)
XLA Modules:
  0.0 54.0 jit_solution(16799510410961824195)
XLA Ops:
  0.0 53.2 %shard_map.37 = bf16[32,48,128]{2,1,0:T(8,128)(2,1)S(1)} custom-call(bf16[32,48,128]{2,1,0:T(8,128)(2,1)} %q_hbm.1, bf16[32,8192,128]{2,1,0:T(8,128)(2,1)} %bitcast.k_hbm, bf16[32,8192,128]{2,1,0:T(8,128)(2,1)} %bitcast.1.v_hbm), custom_call_target="tpu_custom_call" | custom-call | tf_op jit(solution)/shard_map/pallas_call | solution.py:272
  53.2 0.7 %copy.5 = bf16[32,48,128]{2,1,0:T(8,128)(2,1)} copy(bf16[32,48,128]{2,1,0:T(8,128)(2,1)S(1)} %shard_map.37) | data formatting | bytes 786432

commit v3 on v2

--- a/solution.py
+++ b/solution.py
@@ -10,8 +10,9 @@
 
 MESH = pl.DeviceIdType.MESH
 F32, BF16 = jnp.float32, jnp.bfloat16
-SLOTS = 6
-LAG = 4
+SLOTS = 8
+UNROLL = 4
+LAG = 3
 LEAD = 4
 TILE = 256
 
@@ -24,7 +25,7 @@
     return out
 
 
-def kernel(n, heads_kv, q_hbm, k_hbm, v_hbm, out_ref, qbuf, kbuf, vbuf, s0, s1, h0, h1, m0, m1, l0, l1, mask_ref, part, stat, qsem, ksem, vsem,
+def kernel(n, heads_kv, q_hbm, k_hbm, v_hbm, out_ref, qbuf, kbuf, vbuf, s0, s1, s2, h0, h1, h2, m0, m1, l0, l1, one_ref, mask_ref, part, stat, qsem, ksem, vsem,
            part_send, part_recv, stat_send, stat_recv):
     me = lax.axis_index("sp")
     batch, heads, head = qbuf.shape
@@ -32,7 +33,8 @@
     half = rows // 2
     tiles = half // TILE
     factor = head**-0.5 * math.log2(math.e)
-    groups = batch // 2 - 1
+    groups = batch // UNROLL - 1
+    last = batch - 1
 
     def k_copy(i):
         slot = lax.rem(i, slots)
@@ -65,7 +67,8 @@
     k_copy(0).start()
     for i in range(1, slots):
         k_copy(i).start()
-        v_copy(i - 1).start()
+        if i < slots - 1:
+            v_copy(i - 1).start()
 
     barrier = pltpu.get_barrier_semaphore()
     for off in range(1, n):
@@ -73,6 +76,7 @@
 
     per = heads // heads_kv
     own = lax.broadcasted_iota(jnp.int32, (heads, TILE), 0) // per == lax.rem(lax.broadcasted_iota(jnp.int32, (heads, TILE), 1), heads_kv)
+    one_ref[...] = jnp.ones_like(one_ref)
     mask_ref[...] = jnp.where(own, 1.0, 0.0).astype(BF16)
     kind = lax.rem(lax.broadcasted_iota(jnp.int32, (8, TILE), 1), heads_kv)
     lane = lax.broadcasted_iota(jnp.int32, (8, 128), 1)
@@ -100,7 +104,7 @@
         for x in range(2):
             h_ref[x] = jnp.maximum(top[x][:, :128], top[x][:, 128:])
 
-    def weigh(i, s_ref, h_ref, m_ref, l_ref):
+    def weigh(i, s_ref, h_ref, m_ref, l_ref, alone=False):
         slot = lax.rem(i, slots)
         high = [lane_fold(h_ref[x], kind[:, :128], heads_kv, jnp.max, -jnp.inf) for x in range(2)]
         for x in range(2):
@@ -124,7 +128,7 @@
             acc[c % 2] = o if acc[c % 2] is None else acc[c % 2] + o
             if c % 2:
                 yield
-        o = acc[0] + acc[1]
+        o = acc[0] + (acc[1] * one_ref[...] if alone else acc[1])
         part[me, i] = (o[:heads, :head] + o[heads:, head:]).astype(BF16)
         for x in range(2):
             l_ref[x] = sums[x][:, :128] + sums[x][:, 128:]
@@ -199,64 +203,82 @@
     run(scores(0, s0, h0))
     pl.semaphore_wait(barrier, n - 1)
 
+    sets = ((s0, h0, m0, l0), (s1, h1, m1, l1))
+
     def fetch(i):
-        for copy, later in ((k_copy, i + slots), (v_copy, i + slots - 1)):
+        for copy, later in ((k_copy, i + slots), (v_copy, i + slots - 2)):
             @pl.when(later < batch)
             def _():
                 copy(later).start()
 
     def body(full, j, _):
-        i = 2 * j
-        fetch(i)
-        extra = []
+        first = UNROLL * j
+        extra = [()] * UNROLL
         if full:
-            wait_arrivals(j - LAG, 2 * (j - LAG), 2)
-            wait_sent(j - LAG, 2 * (j - LAG), 2)
-            send(j - 2, 2 * (j - 2), 2)
-            extra = [combine(2 * (j - LAG)), combine(2 * (j - LAG) + 1)]
+            g = j - LAG
+            wait_arrivals(g, UNROLL * g, UNROLL)
+            wait_sent(g, UNROLL * g, UNROLL)
+            send(j - 2, UNROLL * (j - 2), UNROLL)
+            extra = [(combine(UNROLL * g + u),) for u in range(UNROLL)]
         else:
             @pl.when(j >= 2)
             def _():
-                send(j - 2, 2 * (j - 2), 2)
-
-        k_copy(i + 1).wait()
-        v_copy(i).wait()
-        block(scores(i + 1, s1, h1), weigh(i, s0, h0, m0, l0), settle(lax.max(i - 1, 0), m1, l1), *extra[:1])
-        fetch(i + 1)
-        k_copy(i + 2).wait()
-        v_copy(i + 1).wait()
-        block(scores(i + 2, s0, h0), weigh(i + 1, s1, h1, m1, l1), settle(i, m0, l0), *extra[1:])
+                send(j - 2, UNROLL * (j - 2), UNROLL)
+
+        together = UNROLL if full else UNROLL // 2
+        for u in range(UNROLL):
+            i = first + u
+            fetch(i)
+            if u % together == 0:
+                for w in range(together):
+                    k_copy(i + w + 1).wait()
+                    v_copy(i + w).wait()
+            now, then = sets[u % 2], sets[(u + 1) % 2]
+            block(scores(i + 1, *then[:2]), weigh(i, *now), settle(lax.max(i - 1, 0), *then[2:]), *extra[u])
         return 0
+
+    def whole(g):
+        return g, UNROLL * g, UNROLL
 
     lax.fori_loop(0, LAG, functools.partial(body, False), 0)
     lax.fori_loop(LAG, groups, functools.partial(body, True), 0)
-    last = batch - 1
-    before = (groups - 2, 2 * (groups - 2), 2)
-    sent = [(groups - 1, 2 * (groups - 1), 2), (groups, last - 1, 1), (groups + 1, last, 1)]
+    tail = [(groups, last - 3, 3), (groups + 1, last, 1)]
+    send(*whole(groups - 2))
+    wait_arrivals(*whole(groups - LAG))
+    wait_sent(*whole(groups - LAG))
+    k_copy(last - 2).wait()
+    v_copy(last - 3).wait()
+    old = [combine(UNROLL * (groups - LAG) + u) for u in range(UNROLL)]
+    block(scores(last - 2, s1, h1), weigh(last - 3, s0, h0, m0, l0), settle(last - 4, m1, l1), *old[:2])
+    send(*whole(groups - 1))
+    k_copy(last - 1).wait()
     k_copy(last).wait()
-    run(scores(last, s1, h1), settle(last - 2, m1, l1))
-    send(*before)
-    send(*sent[0])
+    run(scores(last - 1, s0, h0), settle(last - 3, m0, l0), old[2])
+    run(scores(last, s2, h2), old[3])
+    v_copy(last - 2).wait()
+    run(weigh(last - 2, s1, h1, m1, l1, True))
     v_copy(last - 1).wait()
-    run(weigh(last - 1, s0, h0, m0, l0))
+    run(weigh(last - 1, s0, h0, m0, l0, True), settle(last - 2, m1, l1))
     run(settle(last - 1, m0, l0))
-    send(*sent[1])
+    send(*tail[0])
+    final = weigh(last, s2, h2, m1, l1, True)
+    next(final)
     v_copy(last).wait()
-    run(weigh(last, s1, h1, m1, l1))
+    run(final)
     run(settle(last, m1, l1))
-    send(*sent[2])
+    send(*tail[1])
 
     def rest(g, _):
-        wait_arrivals(g, 2 * g, 2)
-        wait_sent(g, 2 * g, 2)
-        run(combine(2 * g), combine(2 * g + 1))
+        wait_arrivals(*whole(g))
+        wait_sent(*whole(g))
+        run(*[combine(UNROLL * g + u) for u in range(UNROLL)])
         return 0
 
-    lax.fori_loop(groups - LAG, groups, rest, 0)
-    for s in sent[1:]:
+    lax.fori_loop(groups - LAG + 1, groups, rest, 0)
+    for s in tail:
         wait_arrivals(*s)
-        run(combine(s[1]))
-    for s in sent[1:]:
+        run(*[combine(s[1] + u) for u in range(s[2])])
+    for s in tail:
         wait_sent(*s)
 
 
@@ -267,7 +289,7 @@
         batch, heads, head = q.shape
         tokens, heads_kv = k.shape[1:3]
         rows = tokens * heads_kv
-        groups = batch // 2 + 1
+        groups = batch // UNROLL + 1
         any_spec = pl.BlockSpec(memory_space=pl.ANY)
         return pl.pallas_call(
             functools.partial(kernel, n, heads_kv),
@@ -278,9 +300,9 @@
                 pltpu.VMEM((batch, heads, head), BF16),
                 pltpu.VMEM((SLOTS, rows, head), BF16),
                 pltpu.VMEM((SLOTS, rows, head), BF16),
-                pltpu.VMEM((2, 16, rows // 2), F32),
-                pltpu.VMEM((2, 16, rows // 2), F32),
-                *[pltpu.VMEM((2, 8, 128), F32)] * 6,
+                *[pltpu.VMEM((2, 16, rows // 2), F32)] * 3,
+                *[pltpu.VMEM((2, 8, 128), F32)] * 7,
+                pltpu.VMEM((2 * heads, TILE), F32),
                 pltpu.VMEM((heads, TILE), BF16),
                 pltpu.VMEM((n, batch, heads, head), BF16),
                 pltpu.VMEM((n, batch, 8, 128), F32),
@@ -292,7 +314,7 @@
                 pltpu.SemaphoreType.DMA((groups, n - 1)),
                 pltpu.SemaphoreType.DMA((groups, n - 1)),
             ],
-            compiler_params=pltpu.CompilerParams(collective_id=0, has_side_effects=True, vmem_limit_bytes=48 * 2**20),
+            compiler_params=pltpu.CompilerParams(collective_id=0, has_side_effects=True, vmem_limit_bytes=52 * 2**20),
         )(pltpu.with_memory_space_constraint(q, pltpu.HBM), k.reshape(batch, rows, head), v.reshape(batch, rows, head))
 
     return jax.shard_map(

time: 54 us -> 55.9 us (1.035)
  Pallas kernels: 53.2 us -> 55.1 us
    pallas_call x1, Pallas kernels: 53.2 us -> 55.1 us  [step(): pl.pallas_call(functools.partial(kernel, n, heads_kv), out_shape=pltpu.VM...]
where the time goes in v3:
time: 55.9 us; the launch traced here: 55.8 us
  Pallas kernels  55.1 us (99%)
  local copies, waits for them, and re-layouts  0.75 us (1%)
    pallas_call x1, Pallas kernels, step(): pl.pallas_call(functools.partial(kernel, n, heads_kv), out_shape=pltpu.VM...  55.1 us

profile of v3, /device:TPU:112, one launch (start us, length us, event | category | flops | bytes accessed | tf_op | source)
XLA Modules:
  0.0 55.8 jit_solution(11403148266695862037)
XLA Ops:
  0.0 55.1 %shard_map.37 = bf16[32,48,128]{2,1,0:T(8,128)(2,1)S(1)} custom-call(bf16[32,48,128]{2,1,0:T(8,128)(2,1)} %q_hbm.1, bf16[32,8192,128]{2,1,0:T(8,128)(2,1)} %bitcast.k_hbm, bf16[32,8192,128]{2,1,0:T(8,128)(2,1)} %bitcast.1.v_hbm), custom_call_target="tpu_custom_call" | custom-call | tf_op jit(solution)/shard_map/pallas_call | solution.py:294
  55.1 0.7 %copy.5 = bf16[32,48,128]{2,1,0:T(8,128)(2,1)} copy(bf16[32,48,128]{2,1,0:T(8,128)(2,1)S(1)} %shard_map.37) | data formatting | bytes 786432

commit v4 on v2

--- a/solution.py
+++ b/solution.py
@@ -10,7 +10,7 @@
 
 MESH = pl.DeviceIdType.MESH
 F32, BF16 = jnp.float32, jnp.bfloat16
-SLOTS = 6
+SLOTS = 4
 LAG = 4
 LEAD = 4
 TILE = 256
@@ -24,7 +24,7 @@
     return out
 
 
-def kernel(n, heads_kv, q_hbm, k_hbm, v_hbm, out_ref, qbuf, kbuf, vbuf, s0, s1, h0, h1, m0, m1, l0, l1, mask_ref, part, stat, qsem, ksem, vsem,
+def kernel(n, heads_kv, q_hbm, k_hbm, v_hbm, out_ref, qbuf, kbuf, vbuf, s0, s1, h0, h1, m0, m1, l0, l1, one_ref, mask_ref, part, stat, qsem, ksem, vsem,
            part_send, part_recv, stat_send, stat_recv):
     me = lax.axis_index("sp")
     batch, heads, head = qbuf.shape
@@ -63,9 +63,6 @@
     q_copy = pltpu.make_async_copy(q_hbm, qbuf, qsem)
     q_copy.start()
     k_copy(0).start()
-    for i in range(1, slots):
-        k_copy(i).start()
-        v_copy(i - 1).start()
 
     barrier = pltpu.get_barrier_semaphore()
     for off in range(1, n):
@@ -73,6 +70,7 @@
 
     per = heads // heads_kv
     own = lax.broadcasted_iota(jnp.int32, (heads, TILE), 0) // per == lax.rem(lax.broadcasted_iota(jnp.int32, (heads, TILE), 1), heads_kv)
+    one_ref[...] = jnp.ones_like(one_ref)
     mask_ref[...] = jnp.where(own, 1.0, 0.0).astype(BF16)
     kind = lax.rem(lax.broadcasted_iota(jnp.int32, (8, TILE), 1), heads_kv)
     lane = lax.broadcasted_iota(jnp.int32, (8, 128), 1)
@@ -100,7 +98,7 @@
         for x in range(2):
             h_ref[x] = jnp.maximum(top[x][:, :128], top[x][:, 128:])
 
-    def weigh(i, s_ref, h_ref, m_ref, l_ref):
+    def weigh(i, s_ref, h_ref, m_ref, l_ref, alone=False):
         slot = lax.rem(i, slots)
         high = [lane_fold(h_ref[x], kind[:, :128], heads_kv, jnp.max, -jnp.inf) for x in range(2)]
         for x in range(2):
@@ -124,7 +122,7 @@
             acc[c % 2] = o if acc[c % 2] is None else acc[c % 2] + o
             if c % 2:
                 yield
-        o = acc[0] + acc[1]
+        o = acc[0] + (acc[1] * one_ref[...] if alone else acc[1])
         part[me, i] = (o[:heads, :head] + o[heads:, head:]).astype(BF16)
         for x in range(2):
             l_ref[x] = sums[x][:, :128] + sums[x][:, 128:]
@@ -194,9 +192,16 @@
         for c in transfers(g, first, count):
             c.wait_send()
 
+    def pair(i):
+        k_copy(i).start()
+        v_copy(i - 1).start()
+
+    pair(1)
     q_copy.wait()
     k_copy(0).wait()
+    pair(2)
     run(scores(0, s0, h0))
+    pair(3)
     pl.semaphore_wait(barrier, n - 1)
 
     def fetch(i):
@@ -238,11 +243,11 @@
     send(*before)
     send(*sent[0])
     v_copy(last - 1).wait()
-    run(weigh(last - 1, s0, h0, m0, l0))
+    run(weigh(last - 1, s0, h0, m0, l0, True))
     run(settle(last - 1, m0, l0))
     send(*sent[1])
     v_copy(last).wait()
-    run(weigh(last, s1, h1, m1, l1))
+    run(weigh(last, s1, h1, m1, l1, True))
     run(settle(last, m1, l1))
     send(*sent[2])
 
@@ -281,6 +286,7 @@
                 pltpu.VMEM((2, 16, rows // 2), F32),
                 pltpu.VMEM((2, 16, rows // 2), F32),
                 *[pltpu.VMEM((2, 8, 128), F32)] * 6,
+                pltpu.VMEM((2 * heads, TILE), F32),
                 pltpu.VMEM((heads, TILE), BF16),
                 pltpu.VMEM((n, batch, heads, head), BF16),
                 pltpu.VMEM((n, batch, 8, 128), F32),

time: 54 us -> 51.8 us (0.959)
  Pallas kernels: 53.2 us -> 51 us
    pallas_call x1, Pallas kernels: 53.2 us -> 51 us  [step(): pl.pallas_call(functools.partial(kernel, n, heads_kv), out_shape=pltpu.VM...]
where the time goes in v4:
time: 51.8 us
  Pallas kernels  51 us (98%)
  local copies, waits for them, and re-layouts  0.75 us (1%)
    pallas_call x1, Pallas kernels, step(): pl.pallas_call(functools.partial(kernel, n, heads_kv), out_shape=pltpu.VM...  51 us

profile of v4, /device:TPU:112, one launch (start us, length us, event | category | flops | bytes accessed | tf_op | source)
XLA Modules:
  0.0 51.8 jit_solution(14854534582306166703)
XLA Ops:
  0.0 51.0 %shard_map.37 = bf16[32,48,128]{2,1,0:T(8,128)(2,1)S(1)} custom-call(bf16[32,48,128]{2,1,0:T(8,128)(2,1)} %q_hbm.1, bf16[32,8192,128]{2,1,0:T(8,128)(2,1)} %bitcast.k_hbm, bf16[32,8192,128]{2,1,0:T(8,128)(2,1)} %bitcast.1.v_hbm), custom_call_target="tpu_custom_call" | custom-call | tf_op jit(solution)/shard_map/pallas_call | solution.py:277
  51.0 0.7 %copy.5 = bf16[32,48,128]{2,1,0:T(8,128)(2,1)} copy(bf16[32,48,128]{2,1,0:T(8,128)(2,1)S(1)} %shard_map.37) | data formatting | bytes 786432

commit v5 on v4

--- a/solution.py
+++ b/solution.py
@@ -10,7 +10,7 @@
 
 MESH = pl.DeviceIdType.MESH
 F32, BF16 = jnp.float32, jnp.bfloat16
-SLOTS = 4
+SLOTS = 3
 LAG = 4
 LEAD = 4
 TILE = 256
@@ -42,21 +42,25 @@
         slot = lax.rem(i, slots)
         return pltpu.make_async_copy(v_hbm.at[i], vbuf.at[slot], vsem.at[slot])
 
-    def transfers(g, first, count):
+    def pieces(g, src, first, count, row):
+        return (
+            (part.at[src, pl.ds(first, count)], part_send, part_recv),
+            (stat.at[src, row], stat_send, stat_recv),
+        )
+
+    def transfers(g, *which):
         out = []
-        for off in (1, n - 1, *range(2, n - 1)):
+        for off in (*range(2, n - 1), n - 1, 1):
             to = {"sp": lax.rem(me + off, n)}
-            for buf, ssem, rsem in ((part, part_send, part_recv), (stat, stat_send, stat_recv)):
-                ref = buf.at[me, pl.ds(first, count)]
+            for ref, ssem, rsem in pieces(g, me, *which):
                 out.append(pltpu.make_async_remote_copy(ref, ref, ssem.at[g, off - 1], rsem.at[g, off - 1], device_id=to, device_id_type=MESH))
         return out
 
-    def arrivals(g, first, count):
+    def arrivals(g, *which):
         out = []
         for off in range(1, n):
             src = lax.rem(me + n - off, n)
-            for buf, ssem, rsem in ((part, part_send, part_recv), (stat, stat_send, stat_recv)):
-                ref = buf.at[src, pl.ds(first, count)]
+            for ref, ssem, rsem in pieces(g, src, *which):
                 out.append(pltpu.make_async_remote_copy(ref, ref, ssem.at[g, off - 1], rsem.at[g, off - 1], device_id={"sp": src}, device_id_type=MESH))
         return out
 
@@ -127,9 +131,11 @@
         for x in range(2):
             l_ref[x] = sums[x][:, :128] + sums[x][:, 128:]
 
-    def settle(i, m_ref, l_ref):
+    def settle(row, odd, m_ref, l_ref):
         sums = [lane_fold(l_ref[x], kind[:, :128], heads_kv, jnp.sum, 0.0) for x in range(2)]
-        stat[me, i] = jnp.where(lane < 32, m_ref[0], jnp.where(lane < 64, m_ref[1], jnp.where(lane < 96, sums[0], sums[1])))
+        spot = lane & 63
+        new = jnp.where(spot < 16, m_ref[0], jnp.where(spot < 32, m_ref[1], jnp.where(spot < 48, sums[0], sums[1])))
+        stat[me, row] = jnp.where(lane < 64, stat[me, row], new) if odd else new
         yield
 
     def run(*gens):
@@ -158,11 +164,11 @@
                 break
         run(second, *others)
 
-    def combine(i):
-        st = [stat[p, i] for p in range(n)]
+    def combine(i, row, odd):
+        st = [stat[p, row] for p in range(n)]
         top = functools.reduce(jnp.maximum, st)
         scale = [jnp.exp2((s - top) * factor) for s in st]
-        total = sum(w * pltpu.roll(s, 64, 1) for w, s in zip(scale, st))
+        total = sum(w * pltpu.roll(s, 128 - 32, 1) for w, s in zip(scale, st))
         inv = 1.0 / total
         yield
         acc = None
@@ -170,38 +176,44 @@
             w = scale[p] * inv
 
             def col(c):
+                c = c + 64 * odd
                 return jnp.broadcast_to(w[:, c : c + 1], (8, head))
 
-            m01 = jnp.where(low, col(32), col(33))
-            m23 = jnp.where(low, col(34), col(35))
+            m01 = jnp.where(low, col(16), col(17))
+            m23 = jnp.where(low, col(18), col(19))
             full = jnp.concatenate([col(0), m01, col(1), col(2), m23, col(3)], 0)
             term = part[p, i].astype(F32) * full
             acc = term if acc is None else acc + term
             yield
         out_ref[i] = acc.astype(BF16)
 
-    def wait_arrivals(g, first, count):
-        for c in arrivals(g, first, count):
+    def wait_arrivals(*which):
+        for c in arrivals(*which):
             c.wait_recv()
 
-    def send(g, first, count):
-        for c in transfers(g, first, count):
+    def send(*which):
+        for c in transfers(*which):
             c.start()
 
-    def wait_sent(g, first, count):
-        for c in transfers(g, first, count):
+    def wait_sent(*which):
+        for c in transfers(*which):
             c.wait_send()
 
-    def pair(i):
-        k_copy(i).start()
-        v_copy(i - 1).start()
-
-    pair(1)
+    pl.delay(150)
+    k_copy(1).start()
+    pl.delay(300)
+    v_copy(0).start()
+    pl.delay(400)
+    k_copy(2).start()
     q_copy.wait()
     k_copy(0).wait()
-    pair(2)
-    run(scores(0, s0, h0))
-    pair(3)
+
+    def second():
+        for _ in range(4):
+            yield
+        v_copy(1).start()
+
+    run(scores(0, s0, h0), second())
     pl.semaphore_wait(barrier, n - 1)
 
     def fetch(i):
@@ -210,58 +222,65 @@
             def _():
                 copy(later).start()
 
+    def pair(g):
+        return g, 2 * g, 2, g
+
+    def combine_pair(g):
+        return [combine(2 * g, g, 0), combine(2 * g + 1, g, 1)]
+
     def body(full, j, _):
         i = 2 * j
         fetch(i)
         extra = []
         if full:
-            wait_arrivals(j - LAG, 2 * (j - LAG), 2)
-            wait_sent(j - LAG, 2 * (j - LAG), 2)
-            send(j - 2, 2 * (j - 2), 2)
-            extra = [combine(2 * (j - LAG)), combine(2 * (j - LAG) + 1)]
-        else:
-            @pl.when(j >= 2)
-            def _():
-                send(j - 2, 2 * (j - 2), 2)
-
+            wait_arrivals(*pair(j - LAG))
+            wait_sent(*pair(j - LAG))
+            extra = combine_pair(j - LAG)
         k_copy(i + 1).wait()
         v_copy(i).wait()
-        block(scores(i + 1, s1, h1), weigh(i, s0, h0, m0, l0), settle(lax.max(i - 1, 0), m1, l1), *extra[:1])
+        block(scores(i + 1, s1, h1), weigh(i, s0, h0, m0, l0), settle(lax.max(j - 1, 0), 1, m1, l1), *extra[:1])
         fetch(i + 1)
+        if full:
+            send(*pair(j - 1))
+        else:
+            @pl.when(j >= 1)
+            def _():
+                send(*pair(j - 1))
+
         k_copy(i + 2).wait()
         v_copy(i + 1).wait()
-        block(scores(i + 2, s0, h0), weigh(i + 1, s1, h1, m1, l1), settle(i, m0, l0), *extra[1:])
+        block(scores(i + 2, s0, h0), weigh(i + 1, s1, h1, m1, l1), settle(j, 0, m0, l0), *extra[1:])
         return 0
 
     lax.fori_loop(0, LAG, functools.partial(body, False), 0)
     lax.fori_loop(LAG, groups, functools.partial(body, True), 0)
     last = batch - 1
-    before = (groups - 2, 2 * (groups - 2), 2)
-    sent = [(groups - 1, 2 * (groups - 1), 2), (groups, last - 1, 1), (groups + 1, last, 1)]
+    tail = [pair(groups - 1), (groups, last - 1, 1, groups), (groups + 1, last, 1, groups + 1)]
     k_copy(last).wait()
-    run(scores(last, s1, h1), settle(last - 2, m1, l1))
-    send(*before)
-    send(*sent[0])
+    run(settle(groups - 1, 1, m1, l1), scores(last, s1, h1))
+    send(*tail[0])
     v_copy(last - 1).wait()
     run(weigh(last - 1, s0, h0, m0, l0, True))
-    run(settle(last - 1, m0, l0))
-    send(*sent[1])
+    run(settle(groups, 0, m0, l0))
+    send(*tail[1])
+    final = weigh(last, s1, h1, m1, l1, True)
+    next(final)
     v_copy(last).wait()
-    run(weigh(last, s1, h1, m1, l1, True))
-    run(settle(last, m1, l1))
-    send(*sent[2])
+    run(final)
+    run(settle(groups + 1, 0, m1, l1))
+    send(*tail[2])
 
     def rest(g, _):
-        wait_arrivals(g, 2 * g, 2)
-        wait_sent(g, 2 * g, 2)
-        run(combine(2 * g), combine(2 * g + 1))
+        wait_arrivals(*pair(g))
+        wait_sent(*pair(g))
+        run(*combine_pair(g))
         return 0
 
     lax.fori_loop(groups - LAG, groups, rest, 0)
-    for s in sent[1:]:
+    for s in tail[1:]:
         wait_arrivals(*s)
-        run(combine(s[1]))
-    for s in sent[1:]:
+        run(combine(s[1], s[3], 0))
+    for s in tail[1:]:
         wait_sent(*s)
 
 
@@ -289,7 +308,7 @@
                 pltpu.VMEM((2 * heads, TILE), F32),
                 pltpu.VMEM((heads, TILE), BF16),
                 pltpu.VMEM((n, batch, heads, head), BF16),
-                pltpu.VMEM((n, batch, 8, 128), F32),
+                pltpu.VMEM((n, groups, 8, 128), F32),
                 pltpu.SemaphoreType.DMA,
                 pltpu.SemaphoreType.DMA((SLOTS,)),
                 pltpu.SemaphoreType.DMA((SLOTS,)),

time: 51.8 us -> 50.1 us (0.967)
  Pallas kernels: 51 us -> 49.3 us
    pallas_call x1, Pallas kernels: 51 us -> 49.3 us  [step(): pl.pallas_call(functools.partial(kernel, n, heads_kv), out_shape=pltpu.VM...]
where the time goes in v5:
time: 50.1 us
  Pallas kernels  49.3 us (98%)
  local copies, waits for them, and re-layouts  0.75 us (1%)
    pallas_call x1, Pallas kernels, step(): pl.pallas_call(functools.partial(kernel, n, heads_kv), out_shape=pltpu.VM...  49.3 us

profile of v5, /device:TPU:112, one launch (start us, length us, event | category | flops | bytes accessed | tf_op | source)
XLA Modules:
  0.0 50.1 jit_solution(14079241751186028636)
XLA Ops:
  0.0 49.3 %shard_map.37 = bf16[32,48,128]{2,1,0:T(8,128)(2,1)S(1)} custom-call(bf16[32,48,128]{2,1,0:T(8,128)(2,1)} %q_hbm.1, bf16[32,8192,128]{2,1,0:T(8,128)(2,1)} %bitcast.k_hbm, bf16[32,8192,128]{2,1,0:T(8,128)(2,1)} %bitcast.1.v_hbm), custom_call_target="tpu_custom_call" | custom-call | tf_op jit(solution)/shard_map/pallas_call | solution.py:296
  49.3 0.7 %copy.5 = bf16[32,48,128]{2,1,0:T(8,128)(2,1)} copy(bf16[32,48,128]{2,1,0:T(8,128)(2,1)S(1)} %shard_map.37) | data formatting | bytes 786432

commit v6 on v5

--- a/solution.py
+++ b/solution.py
@@ -199,17 +199,17 @@
         for c in transfers(*which):
             c.wait_send()
 
-    pl.delay(150)
+    pl.delay(250)
     k_copy(1).start()
-    pl.delay(300)
+    pl.delay(500)
     v_copy(0).start()
-    pl.delay(400)
+    pl.delay(600)
     k_copy(2).start()
     q_copy.wait()
     k_copy(0).wait()
 
     def second():
-        for _ in range(4):
+        for _ in range(3):
             yield
         v_copy(1).start()
 
@@ -256,15 +256,15 @@
     lax.fori_loop(LAG, groups, functools.partial(body, True), 0)
     last = batch - 1
     tail = [pair(groups - 1), (groups, last - 1, 1, groups), (groups + 1, last, 1, groups + 1)]
+    run(settle(groups - 1, 1, m1, l1))
+    send(*tail[0])
     k_copy(last).wait()
-    run(settle(groups - 1, 1, m1, l1), scores(last, s1, h1))
-    send(*tail[0])
     v_copy(last - 1).wait()
-    run(weigh(last - 1, s0, h0, m0, l0, True))
+    block(scores(last, s1, h1), weigh(last - 1, s0, h0, m0, l0))
+    final = weigh(last, s1, h1, m1, l1, True)
+    next(final)
     run(settle(groups, 0, m0, l0))
     send(*tail[1])
-    final = weigh(last, s1, h1, m1, l1, True)
-    next(final)
     v_copy(last).wait()
     run(final)
     run(settle(groups + 1, 0, m1, l1))

time: 50.1 us -> 49.8 us (level)
  no operation moved by 1% of the time
where the time goes in v6:
time: 49.8 us
  Pallas kernels  49 us (98%)
  local copies, waits for them, and re-layouts  0.75 us (2%)
    pallas_call x1, Pallas kernels, step(): pl.pallas_call(functools.partial(kernel, n, heads_kv), out_shape=pltpu.VM...  49 us

profile of v6, /device:TPU:112, one launch (start us, length us, event | category | flops | bytes accessed | tf_op | source)
XLA Modules:
  0.0 49.8 jit_solution(5841456967359888329)
XLA Ops:
  0.0 49.0 %shard_map.37 = bf16[32,48,128]{2,1,0:T(8,128)(2,1)S(1)} custom-call(bf16[32,48,128]{2,1,0:T(8,128)(2,1)} %q_hbm.1, bf16[32,8192,128]{2,1,0:T(8,128)(2,1)} %bitcast.k_hbm, bf16[32,8192,128]{2,1,0:T(8,128)(2,1)} %bitcast.1.v_hbm), custom_call_target="tpu_custom_call" | custom-call | tf_op jit(solution)/shard_map/pallas_call | solution.py:296
  49.0 0.7 %copy.5 = bf16[32,48,128]{2,1,0:T(8,128)(2,1)} copy(bf16[32,48,128]{2,1,0:T(8,128)(2,1)S(1)} %shard_map.37) | data formatting | bytes 786432

commit v7 on v6

--- a/solution.py
+++ b/solution.py
@@ -13,6 +13,7 @@
 SLOTS = 3
 LAG = 4
 LEAD = 4
+SENDS, ARRIVALS = 8, 9
 TILE = 256
 
 
@@ -42,6 +43,9 @@
         slot = lax.rem(i, slots)
         return pltpu.make_async_copy(v_hbm.at[i], vbuf.at[slot], vsem.at[slot])
 
+    def turn(g, ring):
+        return g % ring if isinstance(g, int) else lax.rem(g, ring)
+
     def pieces(g, src, first, count, row):
         return (
             (part.at[src, pl.ds(first, count)], part_send, part_recv),
@@ -53,7 +57,7 @@
         for off in (*range(2, n - 1), n - 1, 1):
             to = {"sp": lax.rem(me + off, n)}
             for ref, ssem, rsem in pieces(g, me, *which):
-                out.append(pltpu.make_async_remote_copy(ref, ref, ssem.at[g, off - 1], rsem.at[g, off - 1], device_id=to, device_id_type=MESH))
+                out.append(pltpu.make_async_remote_copy(ref, ref, ssem.at[turn(g, SENDS), off - 1], rsem.at[turn(g, ARRIVALS), off - 1], device_id=to, device_id_type=MESH))
         return out
 
     def arrivals(g, *which):
@@ -61,7 +65,7 @@
         for off in range(1, n):
             src = lax.rem(me + n - off, n)
             for ref, ssem, rsem in pieces(g, src, *which):
-                out.append(pltpu.make_async_remote_copy(ref, ref, ssem.at[g, off - 1], rsem.at[g, off - 1], device_id={"sp": src}, device_id_type=MESH))
+                out.append(pltpu.make_async_remote_copy(ref, ref, ssem.at[turn(g, SENDS), off - 1], rsem.at[turn(g, ARRIVALS), off - 1], device_id={"sp": src}, device_id_type=MESH))
         return out
 
     q_copy = pltpu.make_async_copy(q_hbm, qbuf, qsem)
@@ -312,10 +316,10 @@
                 pltpu.SemaphoreType.DMA,
                 pltpu.SemaphoreType.DMA((SLOTS,)),
                 pltpu.SemaphoreType.DMA((SLOTS,)),
-                pltpu.SemaphoreType.DMA((groups, n - 1)),
-                pltpu.SemaphoreType.DMA((groups, n - 1)),
-                pltpu.SemaphoreType.DMA((groups, n - 1)),
-                pltpu.SemaphoreType.DMA((groups, n - 1)),
+                pltpu.SemaphoreType.DMA((SENDS, n - 1)),
+                pltpu.SemaphoreType.DMA((ARRIVALS, n - 1)),
+                pltpu.SemaphoreType.DMA((SENDS, n - 1)),
+                pltpu.SemaphoreType.DMA((ARRIVALS, n - 1)),
             ],
             compiler_params=pltpu.CompilerParams(collective_id=0, has_side_effects=True, vmem_limit_bytes=48 * 2**20),
         )(pltpu.with_memory_space_constraint(q, pltpu.HBM), k.reshape(batch, rows, head), v.reshape(batch, rows, head))

time: 49.8 us -> 48.9 us (0.982)
  Pallas kernels: 49 us -> 48.1 us
    pallas_call x1, Pallas kernels: 49 us -> 48.1 us  [step(): pl.pallas_call(functools.partial(kernel, n, heads_kv), out_shape=pltpu.VM...]
where the time goes in v7:
time: 48.9 us; the launch traced here: 48.8 us
  Pallas kernels  48.1 us (98%)
  local copies, waits for them, and re-layouts  0.75 us (2%)
    pallas_call x1, Pallas kernels, step(): pl.pallas_call(functools.partial(kernel, n, heads_kv), out_shape=pltpu.VM...  48.1 us

profile of v7, /device:TPU:112, one launch (start us, length us, event | category | flops | bytes accessed | tf_op | source)
XLA Modules:
  0.0 48.8 jit_solution(302720066432313156)
XLA Ops:
  0.0 48.1 %shard_map.37 = bf16[32,48,128]{2,1,0:T(8,128)(2,1)S(1)} custom-call(bf16[32,48,128]{2,1,0:T(8,128)(2,1)} %q_hbm.1, bf16[32,8192,128]{2,1,0:T(8,128)(2,1)} %bitcast.k_hbm, bf16[32,8192,128]{2,1,0:T(8,128)(2,1)} %bitcast.1.v_hbm), custom_call_target="tpu_custom_call" | custom-call | tf_op jit(solution)/shard_map/pallas_call | solution.py:300
  48.1 0.7 %copy.5 = bf16[32,48,128]{2,1,0:T(8,128)(2,1)} copy(bf16[32,48,128]{2,1,0:T(8,128)(2,1)S(1)} %shard_map.37) | data formatting | bytes 786432
